TPU v7x, 32 devices: a whole 2x2x4 slice. The times are simulated.
32 devices in a mesh: vocab: 8 (over z, y), batch: 4 (over x, core).
Axes of the slice: x: 2, y: 2, z: 4, core: 2. Of those that a mesh axis runs over, the one named last changes fastest.
Arguments:
- latent_state_rows: bfloat16 [64, 8192], P('batch', 'vocab'), may hold values from -90 to 90
- closing_rescale_coeffs: bfloat16 [8192], replicated, may hold values from 0.5 to 1.5
- output_projection_matrix: bfloat16 [8192, 131072], P(None, ('vocab', 'batch')), may hold values from -3.7565048 to 3.7565048
- config_heat_values: float32 [16], replicated, may hold values from 0.7 to 1.4
- sequence_config_choice: int32 [64], replicated, may hold values from 0 to 15
- ranked_choice_ids: int32 [64, 128], replicated, may hold values from 0 to 131071
- keep_count: int32 [64], replicated, may hold values from 2 to 128
Outputs:
- log_norm: float32 [64], P('batch')
- kept_mass: float32 [64], P('batch')
- renormed: float32 [64, 128], P('batch')
All inputs are finite; a program needn't handle non-finite values.
Results may differ from a plain program's by a relative error of at most 0.0048.
Values may be sent and summed in bfloat16 or wider, within the bound.
No kernel may reach another device: no remote copies, remote signals or barrier semaphores. Data moves between devices by JAX's collectives and lax.ppermute only.
A program may use at most 128 MiB of HBM per device.

v0:
```python
import jax
import jax.numpy as jnp
from jax import lax
from jax.sharding import PartitionSpec as P

epsilon = 1e-06


def normalize(values, gain_part, mean_square):
    factor = lax.rsqrt(mean_square + epsilon)
    return (values * factor[:, None] * gain_part[None, :]).astype(jnp.bfloat16)


def rows_normed(raw_rows, gain_full):
    values = raw_rows.astype(jnp.float32)
    return normalize(values, gain_full, jnp.mean(values * values, axis=1))


def local(
    latent_state_rows,
    closing_rescale_coeffs,
    output_projection_matrix,
    config_heat_values,
    sequence_config_choice,
    ranked_choice_ids,
    keep_count,
):
    group_rows = latent_state_rows.shape[0]
    col_count = output_projection_matrix.shape[1]
    batch_count = lax.axis_size("batch")
    vocab_pos = lax.axis_index("vocab")
    batch_pos = lax.axis_index("batch")
    gain_full = closing_rescale_coeffs.astype(jnp.float32)
    wide_rows = lax.all_gather(latent_state_rows, "vocab", axis=1, tiled=True)
    unnormalized_scores = jnp.dot(
        rows_normed(lax.all_gather(wide_rows, "batch", axis=0, tiled=True), gain_full),
        output_projection_matrix,
        preferred_element_type=jnp.float32,
    )
    config_membership = (
        sequence_config_choice[:, None]
        == jnp.arange(config_heat_values.shape[0], dtype=jnp.int32)[None, :]
    ).astype(jnp.float32)
    sequence_heat_values = jnp.sum(config_membership * config_heat_values[None, :], axis=1)
    divided_scores = unnormalized_scores / sequence_heat_values[:, None]
    offset = (vocab_pos * batch_count + batch_pos) * col_count
    local_ids = ranked_choice_ids - offset
    owned = (local_ids >= 0) & (local_ids < col_count)
    picked = jnp.take_along_axis(divided_scores, jnp.clip(local_ids, 0, col_count - 1), axis=1)
    cand_local = jnp.where(owned, picked, jnp.float32(0.0))
    local_top = jnp.max(divided_scores, axis=1)
    first_slot = batch_pos * group_rows
    row_top = lax.pmax(local_top, ("vocab", "batch"))
    row_total = lax.psum(
        jnp.sum(jnp.exp(divided_scores - row_top[:, None]), axis=1), ("vocab", "batch")
    )
    cand_logit = lax.psum(cand_local, ("vocab", "batch"))
    own_top = lax.dynamic_slice_in_dim(row_top, first_slot, group_rows)
    own_total = lax.dynamic_slice_in_dim(row_total, first_slot, group_rows)
    own_cand = lax.dynamic_slice_in_dim(cand_logit, first_slot, group_rows, 0)
    own_cutoff = lax.dynamic_slice_in_dim(keep_count, first_slot, group_rows)
    log_norm = own_top + jnp.log(own_total)
    kept_mask = jnp.arange(own_cand.shape[1], dtype=jnp.int32)[None, :] < own_cutoff[:, None]
    kept_top = jnp.max(jnp.where(kept_mask, own_cand, jnp.float32(-3e38)), axis=1)
    shifted = jnp.where(kept_mask, own_cand - kept_top[:, None], jnp.float32(0.0))
    kept_exp = jnp.where(kept_mask, jnp.exp(shifted), jnp.float32(0.0))
    kept_sum = jnp.sum(kept_exp, axis=1)
    kept_mass = kept_top + jnp.log(kept_sum) - log_norm
    return (log_norm, kept_mass, kept_exp / kept_sum[:, None])


def solution(mesh):
    placed = (P("batch", "vocab"), P(), P(None, ("vocab", "batch")), P(), P(), P(), P())
    return jax.shard_map(
        local,
        mesh=mesh,
        in_specs=placed,
        out_specs=(P("batch"), P("batch"), P("batch", None)),
        check_vma=False,
    )
```

profile of v0, /device:TPU:0, one launch (start us, length us, event | category | flops | bytes accessed | tf_op | source)
XLA Modules:
  0.0 239.7 jit_solution(4070689631893379016)
XLA Ops:
  7.2 0.0 all-gather.2.cloned.1.call-start
  7.2 34.8 %all_gather.6 = bf16[16,8192]{1,0:T(8,128)(2,1)} all-gather(bf16[16,1024]{1,0:T(8,128)(2,1)} %param.7), channel_id=1, replica_groups=mesh['vocab'=8,'batch'=4] {'vocab'}, dimensions={1}, use_global_device_ids=true | all-gather | bytes 294912 | tf_op jit(solution)/shard_map/all_gather | solution.py:34
  42.0 0.0 all-gather.2.cloned.1.call-update
  42.0 0.7 convert_element_type.11
  42.7 0.7 dynamic_slice.14
  43.5 0.8 select_reduce_fusion.1
  44.2 0.8 fusion.7
  45.0 14.8 %all-gather.2.cloned.1.call-done = bf16[64,8192]{1,0:T(8,128)(2,1)} async-done(((bf16[16,8192]{1,0:T(8,128)(2,1)}), bf16[64,8192]{1,0:T(8,128)(2,1)}) %all-gather.2.cloned.1.call-update) | async-done | bytes 1048592 | tf_op jit(solution)/shard_map/all_gather | solution.py:36
  59.8 1.5 fusion
  61.3 23.9 %fusion.10 = (f32[64]{0:T(128)S(1)}, f32[64,4096]{1,0:T(8,128)S(1)}) fusion(f32[64]{0:T(128)S(1)} %select_reduce_fusion.1, bf16[8192,4096]{1,0:T(8,128)(2,1)} %param.9, bf16[64,8192]{1,0:T(8,128)(2,1)} %all-gather.2.cloned.1.call-done, f32[8192]{0:T(1024)S(1)} %convert_element_type.11, f32[64]{0:T(128)S(1)} %add_rsqrt_fusion), kind=kOutput, calls=%fused_computation.25 | convolution fusion | flops 4297588736 | bytes 69239552 | tf_op jit(solution)/shard_map/dot_general | solution.py:35
  85.2 0.0 copy-start
  85.2 65.0 %gather_fusion = f32[8192]{0:T(1024)S(1)} fusion(f32[64,4096]{1,0:T(8,128)S(1)} %get-tuple-element.8, s32[8192]{0:T(1024)S(1)} %fusion.7), kind=kCustom, calls=%fused_computation | custom fusion | bytes 131072 | tf_op jit(solution)/shard_map/jit(take_along_axis)/gather | solution.py:49
  150.3 0.0 copy-done
  150.3 39.3 %pmax.7 = f32[64]{0:T(128)S(1)} all-reduce(f32[64]{0:T(128)S(1)} %get-tuple-element.7), channel_id=1, replica_groups=mesh['vocab'=8,'batch'=4] {'vocab','batch'}, use_global_device_ids=true, to_apply=%region_3.4 | all-reduce | flops 64 | bytes 512 | tf_op jit(solution)/shard_map/pmax | solution.py:53
  189.6 0.3 exponential_reduce_fusion
  189.9 41.3 %all-reduce = (f32[64]{0:T(128)S(1)}, f32[64,128]{1,0:T(8,128)S(1)}) all-reduce(f32[64]{0:T(128)S(1)} %exponential_reduce_fusion, f32[64,128]{1,0:T(8,128)S(1)} %fusion.6), channel_id=1, replica_groups=mesh['vocab'=8,'batch'=4] {'vocab','batch'}, use_global_device_ids=true, to_apply=%region_5.6 | all-reduce | flops 8256 | bytes 66048 | tf_op jit(solution)/shard_map/psum | solution.py:54
  231.2 0.2 select_reduce_fusion
  231.4 0.2 fusion.9
  231.6 0.7 fusion.8
  232.3 0.6 add_subtract_fusion
  (2 shorter events, 0.0 us)
Async XLA Ops:
  7.2 52.6 %all-gather.2.cloned.1.call-start = ((), (), s32[]{:S(2)}) async-start(), calls=%async_computation | async-start | bytes 1310720 | tf_op jit(solution)/shard_map/all_gather | solution.py:36
  85.2 65.0 %copy-start = (s32[64,128]{1,0:T(8,128)S(1)}, s32[64,128]{1,0:T(8,128)}, u32[]{:S(2)}) copy-start(s32[64,128]{1,0:T(8,128)} %param.12) | copy-start | bytes 98308
Sparse Core Ops, SparseCore 0:
  42.1 17.5 all-gather.1
where the time goes:
time: 240 us
  blocking collectives  115 us (48%)
  local copies, waits for them, and re-layouts  65.7 us (27%)
  matrix products  23.9 us (10%)
  waiting for transfers between devices  14.8 us (6%)
  between operations  14.1 us (6%)
  other arithmetic  5.8 us (2%)
    gather x1, local copies, waits for them, and re-layouts, local(): jnp.take_along_axis(divided_scores, jnp.clip(local_ids, 0, col_count - 1)...  65 us
    psum x1, blocking collectives, local(): lax.psum(jnp.sum(jnp.exp(divided_scores - row_top[:, None]), axis=1), ('v...  41.3 us
    pmax x1, blocking collectives, local(): row_top = lax.pmax(local_top, ('vocab', 'batch'))  39.3 us
    all_gather x1, blocking collectives, local(): wide_rows = lax.all_gather(latent_state_rows, 'vocab', axis=1, tiled=True)  34.8 us
    dot_general x1, matrix products, local(): jnp.dot(rows_normed(lax.all_gather(wide_rows, 'batch', axis=0, tiled=True...  23.9 us
    all_gather x1, waiting for transfers between devices, local(): lax.all_gather(wide_rows, 'batch', axis=0, tiled=True)  14.8 us
  transfers between devices with their start and end apart: 1, of which 1 were waited for; matrix products, arithmetic and copies ran while one was open for 1% of the time, Pallas kernels for 0%

commit v1 on v0

--- a/solution.py
+++ b/solution.py
@@ -31,7 +31,14 @@
     vocab_pos = lax.axis_index("vocab")
     batch_pos = lax.axis_index("batch")
     gain_full = closing_rescale_coeffs.astype(jnp.float32)
-    wide_rows = lax.all_gather(latent_state_rows, "vocab", axis=1, tiled=True)
+    ring = [latent_state_rows]
+    for hop in range(7):
+        ring.append(lax.ppermute(ring[-1], "vocab", [(dev, (dev + 1) % 8) for dev in range(8)]))
+    wide_rows = jnp.roll(
+        jnp.concatenate(ring[::-1], axis=1),
+        (lax.axis_index("vocab") + 1) * ring[0].shape[1],
+        axis=1,
+    )
     unnormalized_scores = jnp.dot(
         rows_normed(lax.all_gather(wide_rows, "batch", axis=0, tiled=True), gain_full),
         output_projection_matrix,

time: 240 us -> 252 us (1.050)
  waiting for transfers between devices: 14.8 us -> 56.3 us
  blocking collectives: 115 us -> 80.6 us
  starting transfers between devices: 0.04 us -> 3.1 us
    ppermute x0 -> x7, waiting for transfers between devices: none -> 45.1 us  [local(): lax.ppermute(ring[-1], 'vocab', [(dev, (dev + 1) % 8) for dev in range(8)])]
    all_gather x1 -> x0, blocking collectives: 34.8 us -> none  [local(): wide_rows = lax.all_gather(latent_state_rows, 'vocab', axis=1, tiled=True)]
    all_gather x1, waiting for transfers between devices: 14.8 us -> 11.1 us  [local(): lax.all_gather(wide_rows, 'batch', axis=0, tiled=True)]
    ppermute x0 -> x7, starting transfers between devices: none -> 3.06 us  [local(): lax.ppermute(ring[-1], 'vocab', [(dev, (dev + 1) % 8) for dev in range(8)])]
  transfers between devices with their start and end apart: 1 -> 8, of which waited for: 1 -> 8; matrix products, arithmetic and copies ran while one was open for 1% -> 1% of each run, Pallas kernels for 0% -> 0%
where the time goes in v1:
time: 252 us
  blocking collectives  80.6 us (32%)
  local copies, waits for them, and re-layouts  68.1 us (27%)
  waiting for transfers between devices  56.3 us (22%)
  matrix products  23.9 us (9%)
  between operations  14.2 us (6%)
  other arithmetic  5.8 us (2%)
  starting transfers between devices  3.1 us (1%)
    gather x1, local copies, waits for them, and re-layouts, local(): jnp.take_along_axis(divided_scores, jnp.clip(local_ids, 0, col_count - 1)...  65 us
    ppermute x7, waiting for transfers between devices, local(): lax.ppermute(ring[-1], 'vocab', [(dev, (dev + 1) % 8) for dev in range(8)])  45.1 us
    psum x1, blocking collectives, local(): lax.psum(jnp.sum(jnp.exp(divided_scores - row_top[:, None]), axis=1), ('v...  41.3 us
    pmax x1, blocking collectives, local(): row_top = lax.pmax(local_top, ('vocab', 'batch'))  39.3 us
    dot_general x1, matrix products, local(): jnp.dot(rows_normed(lax.all_gather(wide_rows, 'batch', axis=0, tiled=True...  23.9 us
    all_gather x1, waiting for transfers between devices, local(): lax.all_gather(wide_rows, 'batch', axis=0, tiled=True)  11.1 us
  transfers between devices with their start and end apart: 8, of which 8 were waited for; matrix products, arithmetic and copies ran while one was open for 1% of the time, Pallas kernels for 0%

profile of v1, /device:TPU:0, one launch (start us, length us, event | category | flops | bytes accessed | tf_op | source)
XLA Modules:
  0.0 251.9 jit_solution(12450725803295042937)
XLA Ops:
  7.2 3.0 %collective-permute-start = (bf16[16,1024]{1,0:T(8,128)(2,1)}, bf16[16,1024]{1,0:T(8,128)(2,1)S(1)}, u32[]{:S(2)}, u32[]{:S(2)}) collective-permute-start(bf16[16,1024]{1,0:T(8,128)(2,1)} %param.7), channel_id=1, source_target_pairs={{0,4},{4,8},{8,12},{12,16},{16,20},{20,24},{24,28},{28,0},{1,5},{5... | collective-permute-start | bytes 98312 | tf_op jit(solution)/shard_map/ppermute | solution.py:36
  10.3 5.1 %collective-permute-done = bf16[16,1024]{1,0:T(8,128)(2,1)S(1)} collective-permute-done((bf16[16,1024]{1,0:T(8,128)(2,1)}, bf16[16,1024]{1,0:T(8,128)(2,1)S(1)}, u32[]{:S(2)}, u32[]{:S(2)}) %collective-permute-start) | collective-permute-done | bytes 32800 | tf_op jit(solution)/shard_map/ppermute | solution.py:36
  15.4 6.6 %collective-permute-done.1 = bf16[16,1024]{1,0:T(8,128)(2,1)S(1)} collective-permute-done((bf16[16,1024]{1,0:T(8,128)(2,1)S(1)}, bf16[16,1024]{1,0:T(8,128)(2,1)S(1)}, u32[]{:S(2)}, u32[]{:S(2)}) %collective-permute-start.1) | collective-permute-done | bytes 32800 | tf_op jit(solution)/shard_map/ppermute | solution.py:36
  22.0 6.6 %collective-permute-done.2 = bf16[16,1024]{1,0:T(8,128)(2,1)S(1)} collective-permute-done((bf16[16,1024]{1,0:T(8,128)(2,1)S(1)}, bf16[16,1024]{1,0:T(8,128)(2,1)S(1)}, u32[]{:S(2)}, u32[]{:S(2)}) %collective-permute-start.2) | collective-permute-done | bytes 32800 | tf_op jit(solution)/shard_map/ppermute | solution.py:36
  28.6 6.6 %collective-permute-done.3 = bf16[16,1024]{1,0:T(8,128)(2,1)S(1)} collective-permute-done((bf16[16,1024]{1,0:T(8,128)(2,1)S(1)}, bf16[16,1024]{1,0:T(8,128)(2,1)S(1)}, u32[]{:S(2)}, u32[]{:S(2)}) %collective-permute-start.3) | collective-permute-done | bytes 32800 | tf_op jit(solution)/shard_map/ppermute | solution.py:36
  35.2 6.9 %collective-permute-done.4 = bf16[16,1024]{1,0:T(8,128)(2,1)S(1)} collective-permute-done((bf16[16,1024]{1,0:T(8,128)(2,1)S(1)}, bf16[16,1024]{1,0:T(8,128)(2,1)S(1)}, u32[]{:S(2)}, u32[]{:S(2)}) %collective-permute-start.4) | collective-permute-done | bytes 32800 | tf_op jit(solution)/shard_map/ppermute | solution.py:36
  42.2 6.6 %collective-permute-done.5 = bf16[16,1024]{1,0:T(8,128)(2,1)S(1)} collective-permute-done((bf16[16,1024]{1,0:T(8,128)(2,1)S(1)}, bf16[16,1024]{1,0:T(8,128)(2,1)S(1)}, u32[]{:S(2)}, u32[]{:S(2)}) %collective-permute-start.5) | collective-permute-done | bytes 32800 | tf_op jit(solution)/shard_map/ppermute | solution.py:36
  48.8 6.6 %collective-permute-done.6 = bf16[16,1024]{1,0:T(8,128)(2,1)S(1)} collective-permute-done((bf16[16,1024]{1,0:T(8,128)(2,1)S(1)}, bf16[16,1024]{1,0:T(8,128)(2,1)S(1)}, u32[]{:S(2)}, u32[]{:S(2)}) %collective-permute-start.6) | collective-permute-done | bytes 32800 | tf_op jit(solution)/shard_map/ppermute | solution.py:36
  55.5 0.8 constant_dynamic-update-slice_fusion.8
  56.3 0.8 constant_dynamic-update-slice_fusion
  57.1 0.7 constant_dynamic-slice_fusion
  57.8 0.7 convert_element_type.11
  58.6 0.7 dynamic_slice.19
  59.3 0.8 select_reduce_fusion.1
  60.1 0.8 fusion.7
  60.8 11.1 %all-gather.2.cloned.1.call-done = bf16[64,8192]{1,0:T(8,128)(2,1)} async-done(((bf16[16,8192]{1,0:T(8,128)(2,1)}), bf16[64,8192]{1,0:T(8,128)(2,1)}) %all-gather.2.cloned.1.call-update) | async-done | bytes 1048592 | tf_op jit(solution)/shard_map/all_gather | solution.py:43
  72.0 1.5 fusion
  73.5 23.9 %fusion.10 = (f32[64]{0:T(128)S(1)}, f32[64,4096]{1,0:T(8,128)S(1)}) fusion(f32[64]{0:T(128)S(1)} %select_reduce_fusion.1, bf16[8192,4096]{1,0:T(8,128)(2,1)} %param.9, bf16[64,8192]{1,0:T(8,128)(2,1)} %all-gather.2.cloned.1.call-done, f32[8192]{0:T(1024)S(1)} %convert_element_type.11, f32[64]{0:T(128)S(1)} %add_rsqrt_fusion), kind=kOutput, calls=%fused_computation.42 | convolution fusion | flops 4297588736 | bytes 69239552 | tf_op jit(solution)/shard_map/dot_general | solution.py:42
  97.5 65.0 %gather_fusion = f32[8192]{0:T(1024)S(1)} fusion(f32[64,4096]{1,0:T(8,128)S(1)} %get-tuple-element.8, s32[8192]{0:T(1024)S(1)} %fusion.7), kind=kCustom, calls=%fused_computation | custom fusion | bytes 131072 | tf_op jit(solution)/shard_map/jit(take_along_axis)/gather | solution.py:56
  162.5 39.3 %pmax.7 = f32[64]{0:T(128)S(1)} all-reduce(f32[64]{0:T(128)S(1)} %get-tuple-element.7), channel_id=1, replica_groups=mesh['vocab'=8,'batch'=4] {'vocab','batch'}, use_global_device_ids=true, to_apply=%region_3.4 | all-reduce | flops 64 | bytes 512 | tf_op jit(solution)/shard_map/pmax | solution.py:60
  201.8 0.3 exponential_reduce_fusion
  202.1 41.3 %all-reduce = (f32[64]{0:T(128)S(1)}, f32[64,128]{1,0:T(8,128)S(1)}) all-reduce(f32[64]{0:T(128)S(1)} %exponential_reduce_fusion, f32[64,128]{1,0:T(8,128)S(1)} %fusion.6), channel_id=1, replica_groups=mesh['vocab'=8,'batch'=4] {'vocab','batch'}, use_global_device_ids=true, to_apply=%region_5.6 | all-reduce | flops 8256 | bytes 66048 | tf_op jit(solution)/shard_map/psum | solution.py:61
  243.8 0.7 fusion.8
  244.5 0.6 add_subtract_fusion
  (28 shorter events, 0.5 us)
Async XLA Ops:
  7.2 64.8 %all-gather.2.cloned.1.call-start = ((), (), s32[]{:S(2)}) async-start(), calls=%async_computation | async-start | bytes 1310720 | tf_op jit(solution)/shard_map/all_gather | solution.py:43
  7.2 8.2 %collective-permute-start = (bf16[16,1024]{1,0:T(8,128)(2,1)}, bf16[16,1024]{1,0:T(8,128)(2,1)S(1)}, u32[]{:S(2)}, u32[]{:S(2)}) collective-permute-start(bf16[16,1024]{1,0:T(8,128)(2,1)} %param.7), channel_id=1, source_target_pairs={{0,4},{4,8},{8,12},{12,16},{16,20},{20,24},{24,28},{28,0},{1,5},{5... | collective-permute-start | bytes 98312 | tf_op jit(solution)/shard_map/ppermute | solution.py:36
  15.4 6.6 %collective-permute-start.1 = (bf16[16,1024]{1,0:T(8,128)(2,1)S(1)}, bf16[16,1024]{1,0:T(8,128)(2,1)S(1)}, u32[]{:S(2)}, u32[]{:S(2)}) collective-permute-start(bf16[16,1024]{1,0:T(8,128)(2,1)S(1)} %collective-permute-done), channel_id=1, source_target_pairs={{0,4},{4,8},{8,12},{12,16},{16,20},{20,24},{24,28},{28,0},{1,5},{5... | collective-permute-start | bytes 98312 | tf_op jit(solution)/shard_map/ppermute | solution.py:36
  22.0 6.6 %collective-permute-start.2 = (bf16[16,1024]{1,0:T(8,128)(2,1)S(1)}, bf16[16,1024]{1,0:T(8,128)(2,1)S(1)}, u32[]{:S(2)}, u32[]{:S(2)}) collective-permute-start(bf16[16,1024]{1,0:T(8,128)(2,1)S(1)} %collective-permute-done.1), channel_id=1, source_target_pairs={{0,4},{4,8},{8,12},{12,16},{16,20},{20,24},{24,28},{28,0},{1,5},{5... | collective-permute-start | bytes 98312 | tf_op jit(solution)/shard_map/ppermute | solution.py:36
  28.6 6.6 %collective-permute-start.3 = (bf16[16,1024]{1,0:T(8,128)(2,1)S(1)}, bf16[16,1024]{1,0:T(8,128)(2,1)S(1)}, u32[]{:S(2)}, u32[]{:S(2)}) collective-permute-start(bf16[16,1024]{1,0:T(8,128)(2,1)S(1)} %collective-permute-done.2), channel_id=1, source_target_pairs={{0,4},{4,8},{8,12},{12,16},{16,20},{20,24},{24,28},{28,0},{1,5},{5... | collective-permute-start | bytes 98312 | tf_op jit(solution)/shard_map/ppermute | solution.py:36
  35.2 7.0 %collective-permute-start.4 = (bf16[16,1024]{1,0:T(8,128)(2,1)S(1)}, bf16[16,1024]{1,0:T(8,128)(2,1)S(1)}, u32[]{:S(2)}, u32[]{:S(2)}) collective-permute-start(bf16[16,1024]{1,0:T(8,128)(2,1)S(1)} %collective-permute-done.3), channel_id=1, source_target_pairs={{0,4},{4,8},{8,12},{12,16},{16,20},{20,24},{24,28},{28,0},{1,5},{5... | collective-permute-start | bytes 98312 | tf_op jit(solution)/shard_map/ppermute | solution.py:36
  42.2 6.6 %collective-permute-start.5 = (bf16[16,1024]{1,0:T(8,128)(2,1)S(1)}, bf16[16,1024]{1,0:T(8,128)(2,1)S(1)}, u32[]{:S(2)}, u32[]{:S(2)}) collective-permute-start(bf16[16,1024]{1,0:T(8,128)(2,1)S(1)} %collective-permute-done.4), channel_id=1, source_target_pairs={{0,4},{4,8},{8,12},{12,16},{16,20},{20,24},{24,28},{28,0},{1,5},{5... | collective-permute-start | bytes 98312 | tf_op jit(solution)/shard_map/ppermute | solution.py:36
  48.8 6.6 %collective-permute-start.6 = (bf16[16,1024]{1,0:T(8,128)(2,1)S(1)}, bf16[16,1024]{1,0:T(8,128)(2,1)S(1)}, u32[]{:S(2)}, u32[]{:S(2)}) collective-permute-start(bf16[16,1024]{1,0:T(8,128)(2,1)S(1)} %collective-permute-done.5), channel_id=1, source_target_pairs={{0,4},{4,8},{8,12},{12,16},{16,20},{20,24},{24,28},{28,0},{1,5},{5... | collective-permute-start | bytes 98312 | tf_op jit(solution)/shard_map/ppermute | solution.py:36
  97.4 65.0 %copy-start = (s32[64,128]{1,0:T(8,128)S(1)}, s32[64,128]{1,0:T(8,128)}, u32[]{:S(2)}) copy-start(s32[64,128]{1,0:T(8,128)} %param.12) | copy-start | bytes 98308
Sparse Core Ops, SparseCore 0:
  58.0 13.9 all-gather.1

commit v2 on v0

--- a/solution.py
+++ b/solution.py
@@ -52,7 +52,7 @@
     first_slot = batch_pos * group_rows
     row_top = lax.pmax(local_top, ("vocab", "batch"))
     row_total = lax.psum(
-        jnp.sum(jnp.exp(divided_scores - row_top[:, None]), axis=1), ("vocab", "batch")
+        lax.psum(jnp.sum(jnp.exp(divided_scores - row_top[:, None]), axis=1), "batch"), "vocab"
     )
     cand_logit = lax.psum(cand_local, ("vocab", "batch"))
     own_top = lax.dynamic_slice_in_dim(row_top, first_slot, group_rows)

time: 240 us -> 267 us (1.11)
  blocking collectives: 115 us -> 142 us
    psum x1 -> x3, blocking collectives: 41.3 us -> 66.5 us  [the longest x1 39.4 us: local(): cand_logit = lax.psum(cand_local, ('vocab', 'batch'))]
where the time goes in v2:
time: 267 us
  blocking collectives  142 us (53%)
  local copies, waits for them, and re-layouts  65.7 us (25%)
  matrix products  23.9 us (9%)
  waiting for transfers between devices  14.8 us (6%)
  between operations  14.1 us (5%)
  other arithmetic  5.78 us (2%)
    gather x1, local copies, waits for them, and re-layouts, local(): jnp.take_along_axis(divided_scores, jnp.clip(local_ids, 0, col_count - 1)...  65 us
    pmax x1, blocking collectives, local(): row_top = lax.pmax(local_top, ('vocab', 'batch'))  40.9 us
    psum x1, blocking collectives, local(): cand_logit = lax.psum(cand_local, ('vocab', 'batch'))  39.4 us
    all_gather x1, blocking collectives, local(): wide_rows = lax.all_gather(latent_state_rows, 'vocab', axis=1, tiled=True)  34.8 us
    dot_general x1, matrix products, local(): jnp.dot(rows_normed(lax.all_gather(wide_rows, 'batch', axis=0, tiled=True...  23.9 us
    psum x1, blocking collectives, local(): lax.psum(lax.psum(jnp.sum(jnp.exp(divided_scores - row_top[:, None]), axi...  21.3 us
    all_gather x1, waiting for transfers between devices, local(): lax.all_gather(wide_rows, 'batch', axis=0, tiled=True)  14.8 us
    psum x1, blocking collectives, local(): lax.psum(jnp.sum(jnp.exp(divided_scores - row_top[:, None]), axis=1), 'ba...  5.83 us
  transfers between devices with their start and end apart: 1, of which 1 were waited for; matrix products, arithmetic and copies ran while one was open for 1% of the time, Pallas kernels for 0%

profile of v2, /device:TPU:0, one launch (start us, length us, event | category | flops | bytes accessed | tf_op | source)
XLA Modules:
  0.0 266.6 jit_solution(9997333788093067045)
XLA Ops:
  7.2 0.0 all-gather.2.cloned.1.call-start
  7.2 34.8 %all_gather.6 = bf16[16,8192]{1,0:T(8,128)(2,1)} all-gather(bf16[16,1024]{1,0:T(8,128)(2,1)} %param.7), channel_id=1, replica_groups=mesh['vocab'=8,'batch'=4] {'vocab'}, dimensions={1}, use_global_device_ids=true | all-gather | bytes 294912 | tf_op jit(solution)/shard_map/all_gather | solution.py:34
  42.0 0.0 all-gather.2.cloned.1.call-update
  42.0 0.7 convert_element_type.11
  42.7 0.7 dynamic_slice.14
  43.5 0.8 select_reduce_fusion.1
  44.2 0.8 fusion.7
  45.0 14.8 %all-gather.2.cloned.1.call-done = bf16[64,8192]{1,0:T(8,128)(2,1)} async-done(((bf16[16,8192]{1,0:T(8,128)(2,1)}), bf16[64,8192]{1,0:T(8,128)(2,1)}) %all-gather.2.cloned.1.call-update) | async-done | bytes 1048592 | tf_op jit(solution)/shard_map/all_gather | solution.py:36
  59.8 1.5 fusion
  61.3 23.9 %fusion.10 = (f32[64]{0:T(128)S(1)}, f32[64,4096]{1,0:T(8,128)S(1)}) fusion(f32[64]{0:T(128)S(1)} %select_reduce_fusion.1, bf16[8192,4096]{1,0:T(8,128)(2,1)} %param.9, bf16[64,8192]{1,0:T(8,128)(2,1)} %all-gather.2.cloned.1.call-done, f32[8192]{0:T(1024)S(1)} %convert_element_type.11, f32[64]{0:T(128)S(1)} %add_rsqrt_fusion), kind=kOutput, calls=%fused_computation.25 | convolution fusion | flops 4297588736 | bytes 69239552 | tf_op jit(solution)/shard_map/dot_general | solution.py:35
  85.2 0.0 copy-start
  85.2 65.0 %gather_fusion = f32[8192]{0:T(1024)S(1)} fusion(f32[64,4096]{1,0:T(8,128)S(1)} %get-tuple-element.6, s32[8192]{0:T(1024)S(1)} %fusion.7), kind=kCustom, calls=%fused_computation | custom fusion | bytes 131072 | tf_op jit(solution)/shard_map/jit(take_along_axis)/gather | solution.py:49
  150.3 0.0 copy-done
  150.3 39.4 %psum.23 = f32[64,128]{1,0:T(8,128)S(1)} all-reduce(f32[64,128]{1,0:T(8,128)S(1)} %fusion.6), channel_id=1, replica_groups=mesh['vocab'=8,'batch'=4] {'vocab','batch'}, use_global_device_ids=true, to_apply=%region_7.8 | all-reduce | flops 8192 | bytes 65536 | tf_op jit(solution)/shard_map/psum | solution.py:57
  189.8 0.2 select_reduce_fusion
  189.9 0.2 fusion.9
  190.1 40.9 %pmax.7 = f32[64]{0:T(128)S(1)} all-reduce(f32[64]{0:T(128)S(1)} %get-tuple-element.5), channel_id=1, replica_groups=mesh['vocab'=8,'batch'=4] {'vocab','batch'}, use_global_device_ids=true, to_apply=%region_3.4 | all-reduce | flops 64 | bytes 512 | tf_op jit(solution)/shard_map/pmax | solution.py:53
  231.1 0.3 exponential_reduce_fusion
  231.4 5.8 %psum.21 = f32[64]{0:T(128)S(1)} all-reduce(f32[64]{0:T(128)S(1)} %exponential_reduce_fusion), channel_id=1, replica_groups=mesh['vocab'=8,'batch'=4] {'batch'}, use_global_device_ids=true, to_apply=%region_5.6 | all-reduce | flops 64 | bytes 512 | tf_op jit(solution)/shard_map/psum | solution.py:55
  237.2 21.3 %psum.22 = f32[64]{0:T(128)S(1)} all-reduce(f32[64]{0:T(128)S(1)} %psum.21), channel_id=1, replica_groups=mesh['vocab'=8,'batch'=4] {'vocab'}, use_global_device_ids=true, to_apply=%region_6.7 | all-reduce | flops 64 | bytes 512 | tf_op jit(solution)/shard_map/psum | solution.py:54
  258.5 0.7 fusion.8
  259.2 0.6 add_subtract_fusion
  (2 shorter events, 0.0 us)
Async XLA Ops:
  7.2 52.6 %all-gather.2.cloned.1.call-start = ((), (), s32[]{:S(2)}) async-start(), calls=%async_computation | async-start | bytes 1310720 | tf_op jit(solution)/shard_map/all_gather | solution.py:36
  85.2 65.0 %copy-start = (s32[64,128]{1,0:T(8,128)S(1)}, s32[64,128]{1,0:T(8,128)}, u32[]{:S(2)}) copy-start(s32[64,128]{1,0:T(8,128)} %param.12) | copy-start | bytes 98308
Sparse Core Ops, SparseCore 0:
  42.1 17.5 all-gather.1
